TPU v7x, 32 devices: a whole 2x2x4 slice. The times are simulated.
32 devices in a mesh: expert: 8 (over y, x, core), dp: 4 (over z).
Axes of the slice: x: 2, y: 2, z: 4, core: 2. Of those that a mesh axis runs over, the one named last changes fastest.
Arguments:
- patches: bfloat16 [8192, 1024], P(('expert', 'dp')), may hold values from -6 to 6
- router_weight: bfloat16 [1024, 8], replicated, may hold values from -0.1875 to 0.1875
- router_bias: float32 [8], replicated, may hold values from -1.5 to 1.5
- noise: float32 [8192, 8], P(('expert', 'dp')), may hold values from -5 to 5
- top_experts: int32 [8192, 2], P(('expert', 'dp')), may hold values from 0 to 7, all different within a row; in each aligned block of 256 rows (0 to 255, 256 to 511, ...) at most 80 rows name the same one
- threshold_expert: int32 [8192], P(('expert', 'dp')), may hold values from 0 to 7
- w_in: bfloat16 [8, 1024, 2048], P('expert'), may hold values from -0.1875 to 0.1875
- w_out: bfloat16 [8, 2048, 1024], P('expert'), may hold values from -0.125 to 0.125
- out_grad: bfloat16 [8192, 1024], P(('expert', 'dp')), may hold values from -24 to 24
Outputs:
- patch_grad: bfloat16 [8192, 1024], P(('expert', 'dp'))
- w_in_grad: bfloat16 [8, 1024, 2048], P('expert', None, 'dp')
- w_out_grad: bfloat16 [8, 2048, 1024], P('expert', 'dp')
- router_weight_grad: float32 [1024, 8], replicated
- router_bias_grad: float32 [8], replicated
Inputs may be any that keep to these rules, and one draw needn't show every extreme that they name: `top_experts`: the two experts of a patch differ; among the patches of one device no expert is named more than 80 times.
All inputs are finite; a program needn't handle non-finite values.
Results may differ from a plain program's by a relative error of at most 0.0062.
The roundings to bfloat16 on the way count: a program that leaves them out, or rounds other values in their place, can miss the bound.
Values may be sent and summed in bfloat16 or wider, within the bound.
A program may use at most 128 MiB of HBM per device.

v0:
```python
import jax
import jax.numpy as jnp
from jax import lax
from jax.sharding import PartitionSpec as P

noise_std = 1.0
aux_weight = 1.0
inv_root_two = 0.7071067811865476
inv_root_tau = 0.3989422804014327


def gelu_tanh(values):
    return jax.nn.gelu(values, approximate=True)


def spread_grad(values):
    number = values.shape[0]
    average = jnp.mean(values)
    spread = jnp.mean((values - average) ** 2)
    return (2.0 * (values - average) - 2.0 * spread / average) / (number * average * average)


def expert_local(rows_in, rows_grad, rows_gate, w_first, w_second):
    hidden = jnp.dot(rows_in, w_first, preferred_element_type=jnp.float32)
    active, pullback = jax.vjp(gelu_tanh, hidden)
    active_low = lax.optimization_barrier(active.astype(jnp.bfloat16))
    back_proj = jnp.dot(rows_grad, w_second.T, preferred_element_type=jnp.float32)
    gate_col = rows_gate.astype(jnp.float32)[:, None]
    gate_terms = jnp.sum(back_proj * active_low.astype(jnp.float32), axis=-1)
    hidden_grad = pullback(gate_col * back_proj)[0].astype(jnp.bfloat16)
    scaled_grad = (gate_col * rows_grad.astype(jnp.float32)).astype(jnp.bfloat16)
    first_grad = jnp.dot(rows_in.T, hidden_grad, preferred_element_type=jnp.float32)
    second_grad = jnp.dot(active_low.T, scaled_grad, preferred_element_type=jnp.float32)
    return (first_grad, second_grad, hidden_grad, gate_terms)


def expert_terms(rows_in, rows_grad, rows_gate, w_first, w_second):
    first_grad, second_grad, hidden_grad, gate_terms = expert_local(
        rows_in, rows_grad, rows_gate, w_first, w_second
    )
    rows_back = jnp.dot(hidden_grad, w_first.T, preferred_element_type=jnp.float32)
    return (first_grad, second_grad, rows_back, gate_terms)


def on_device(
    patches, router_weight, router_bias, noise, top_experts, threshold_expert, w_in, w_out, out_grad
):
    tok_rows = patches.shape[0]
    width = patches.shape[1]
    experts = router_weight.shape[1]
    capacity = 5 * tok_rows // (2 * experts)
    slots = experts * capacity
    total_tokens = tok_rows * lax.axis_size("expert") * lax.axis_size("dp")
    logits = jnp.dot(patches, router_weight, preferred_element_type=jnp.float32) + router_bias
    noisy = logits + noise_std * noise
    probs = jax.nn.softmax(noisy, axis=-1)
    expert_ids = lax.broadcasted_iota(jnp.int32, (1, experts), 1)
    thresh_hot = threshold_expert[:, None] == expert_ids
    base = jnp.sum(jnp.where(thresh_hot, noisy, 0.0), axis=-1, keepdims=True)
    zscore = (logits - base) / noise_std
    importance, load = lax.psum(
        (jnp.sum(probs, axis=0), jnp.sum(0.5 * (1.0 + lax.erf(zscore * inv_root_two)), axis=0)),
        ("expert", "dp"),
    )
    top_hot = top_experts[:, :, None] == expert_ids[None]
    gates = jnp.sum(jnp.where(top_hot, probs[:, None, :], 0.0), axis=-1).astype(jnp.bfloat16)
    flat = top_experts.reshape(-1)
    flat_hot = (flat[:, None] == expert_ids).astype(jnp.int32)
    before = jnp.sum((jnp.cumsum(flat_hot, axis=0) - flat_hot) * flat_hot, axis=-1)
    slot_ids = flat * capacity + before
    slot_index = lax.broadcasted_iota(jnp.int32, (slots, 1), 0)
    assign = (slot_index == slot_ids[None, :]).astype(jnp.bfloat16)
    assign_tok = jnp.sum(assign.reshape(slots, tok_rows, 2), axis=-1)
    sent_in = (
        jnp.dot(assign_tok, patches, preferred_element_type=jnp.float32)
        .astype(jnp.bfloat16)
        .reshape(experts, capacity, width)
    )
    sent_grad = (
        jnp.dot(assign_tok, out_grad, preferred_element_type=jnp.float32)
        .astype(jnp.bfloat16)
        .reshape(experts, capacity, width)
    )
    sent_gate = (
        jnp.dot(assign, gates.reshape(-1), preferred_element_type=jnp.float32)
        .astype(jnp.bfloat16)
        .reshape(experts, capacity)
    )
    recv_in, recv_grad, recv_gate = (
        lax.all_to_all(sent_in, "expert", split_axis=0, concat_axis=0, tiled=True),
        lax.all_to_all(sent_grad, "expert", split_axis=0, concat_axis=0, tiled=True),
        lax.all_to_all(sent_gate, "expert", split_axis=0, concat_axis=0, tiled=True),
    )
    rows_in = recv_in.reshape(slots, width)
    rows_grad = recv_grad.reshape(slots, width)
    rows_gate = recv_gate.reshape(slots)
    w_first = w_in[0]
    w_second = w_out[0]
    first_grad, second_grad, rows_back, gate_terms = expert_terms(
        rows_in, rows_grad, rows_gate, w_first, w_second
    )
    first_part, second_part = (
        lax.psum_scatter(first_grad, "dp", scatter_dimension=1, tiled=True),
        lax.psum_scatter(second_grad, "dp", scatter_dimension=0, tiled=True),
    )
    back_rows = rows_back.astype(jnp.bfloat16).reshape(experts, capacity, width)
    back_gate = gate_terms.astype(jnp.bfloat16).reshape(experts, capacity)
    home_rows, home_gate = (
        lax.all_to_all(back_rows, "expert", split_axis=0, concat_axis=0, tiled=True),
        lax.all_to_all(back_gate, "expert", split_axis=0, concat_axis=0, tiled=True),
    )
    expert_back = jnp.dot(
        assign_tok.T, home_rows.reshape(slots, width), preferred_element_type=jnp.float32
    )
    gate_grad = jnp.dot(
        home_gate.reshape(slots), assign, preferred_element_type=jnp.float32
    ).reshape(tok_rows, 2)
    total_weight = aux_weight * total_tokens
    imp_coef = total_weight * spread_grad(importance)
    load_coef = total_weight * spread_grad(load)
    score_grad = jnp.sum(jnp.where(top_hot, gate_grad[:, :, None], 0.0), axis=1) + imp_coef[None, :]
    noisy_grad = probs * (score_grad - jnp.sum(probs * score_grad, axis=-1, keepdims=True))
    z_grad = load_coef[None, :] * inv_root_tau * jnp.exp(-0.5 * zscore * zscore)
    logit_grad = (
        noisy_grad
        + z_grad / noise_std
        - jnp.where(thresh_hot, jnp.sum(z_grad, axis=-1, keepdims=True) / noise_std, 0.0)
    )
    logit_low = logit_grad.astype(jnp.bfloat16)
    router_back = jnp.dot(logit_low, router_weight.T, preferred_element_type=jnp.float32)
    patch_grad = (expert_back + router_back).astype(jnp.bfloat16)
    weight_part = jnp.dot(patches.T, logit_low, preferred_element_type=jnp.float32)
    router_weight_grad, router_bias_grad = lax.psum(
        (weight_part, jnp.sum(logit_grad, axis=0)), ("expert", "dp")
    )
    return (
        patch_grad,
        first_part.astype(jnp.bfloat16)[None],
        second_part.astype(jnp.bfloat16)[None],
        router_weight_grad,
        router_bias_grad,
    )


def solution(mesh):
    placed = (
        P(("expert", "dp"), None),
        P(),
        P(),
        P(("expert", "dp"), None),
        P(("expert", "dp"), None),
        P(("expert", "dp")),
        P("expert", None, None),
        P("expert", None, None),
        P(("expert", "dp"), None),
    )
    return jax.shard_map(
        on_device,
        mesh=mesh,
        in_specs=placed,
        out_specs=(
            P(("expert", "dp"), None),
            P("expert", None, "dp"),
            P("expert", "dp", None),
            P(),
            P(),
        ),
        check_vma=False,
    )
```

profile of v0, /device:TPU:0, one launch (start us, length us, event | category | flops | bytes accessed | tf_op | source)
XLA Modules:
  0.0 399.7 jit_solution(11020807704980809299)
XLA Ops:
  7.2 0.9 copy.39
  8.4 1.1 reduce-window.6
  10.1 0.7 multiply_add_fusion.1
  11.1 1.6 convolution_convert_fusion
  12.7 5.3 %all-to-all-start.2 = ((bf16[8,80,1024]{2,1,0:T(8,128)(2,1)}), bf16[8,80,1024]{2,1,0:T(8,128)(2,1)S(1)}, u32[]{:S(2)}, u32[]{:S(2)}) async-start(bf16[8,80,1024]{2,1,0:T(8,128)(2,1)} %bitcast.6), calls=%async_computation.2 | async-start | bytes 2621440 | tf_op jit(solution)/shard_map/all_to_all | solution.py:90
  18.3 1.6 convolution_convert_fusion.1
  19.9 16.3 %all-to-all-done.2 = bf16[8,80,1024]{2,1,0:T(8,128)(2,1)S(1)} async-done(((bf16[8,80,1024]{2,1,0:T(8,128)(2,1)}), bf16[8,80,1024]{2,1,0:T(8,128)(2,1)S(1)}, u32[]{:S(2)}, u32[]{:S(2)}) %all-to-all-start.2) | async-done | bytes 1310752 | tf_op jit(solution)/shard_map/all_to_all | solution.py:90
  36.2 3.6 all-to-all-start.1
  39.8 1.0 iota_compare_fusion
  40.8 8.1 %multiply_convert_fusion = (bf16[640,2048]{1,0:T(8,128)(2,1)}, f32[640,2048]{1,0:T(8,128)}) fusion(bf16[640,1024]{1,0:T(8,128)(2,1)S(1)} %bitcast.58, bf16[1,1024,2048]{2,1,0:T(8,128)(2,1)} %param.15), kind=kOutput, calls=%fused_computation.10 | convolution fusion | flops 2696151040 | bytes 13369344 | tf_op jit(solution)/shard_map/dot_general | solution.py:24
  48.9 9.0 %all-to-all-done.1 = bf16[8,80,1024]{2,1,0:T(8,128)(2,1)S(1)} async-done(((bf16[8,80,1024]{2,1,0:T(8,128)(2,1)}), bf16[8,80,1024]{2,1,0:T(8,128)(2,1)S(1)}, u32[]{:S(2)}, u32[]{:S(2)}) %all-to-all-start.1) | async-done | bytes 1310752 | tf_op jit(solution)/shard_map/all_to_all | solution.py:91
  57.9 8.8 %multiply_reduce_fusion = (bf16[640]{0:T(1024)(128)(2,1)S(1)}, f32[640,2048]{1,0:T(8,128)}) fusion(bf16[640,2048]{1,0:T(8,128)(2,1)} %get-tuple-element.19, bf16[640,1024]{1,0:T(8,128)(2,1)S(1)} %bitcast.60, bf16[1,2048,1024]{2,1,0:T(8,128)(2,1)} %param.16), kind=kOutput, calls=%fused_computation.9 | convolution fusion | flops 2688286208 | bytes 13370624 | tf_op jit(solution)/shard_map/dot_general | solution.py:27
  66.7 0.7 convert_element_type.106
  67.4 3.3 all-to-all-start.4
  71.3 3.9 all-to-all-done.4
  75.3 0.9 fusion.16
  77.1 7.1 %all_to_all.31 = bf16[8,1,80]{2,1,0:T(2,128)(2,1)S(1)} all-to-all(bf16[8,1,80]{2,1,0:T(2,128)(2,1)S(1)} %all_to_all.25), channel_id=1, replica_groups=mesh['expert'=8,'dp'=4] {'expert'}, dimensions={0} | all-to-all | bytes 2560 | tf_op jit(solution)/shard_map/all_to_all | solution.py:92
  84.3 6.5 %fusion.6 = bf16[640,2048]{1,0:T(8,128)(2,1)S(1)} fusion(f32[640,2048]{1,0:T(8,128)} %get-tuple-element.20, f32[640,2048]{1,0:T(8,128)} %get-tuple-element.22, f32[640]{0:T(1024)S(1)} %reshape.148), kind=kLoop, calls=%fused_computation.8 | loop fusion | flops 27525120 | bytes 13109760 | tf_op jit(solution)/shard_map/convert_element_type | solution.py:30
  90.8 5.7 %fusion.40 = f32[1024,2048]{1,0:T(8,128)} fusion(bf16[640,1024]{1,0:T(8,128)(2,1)S(1)} %bitcast.59, bf16[640,2048]{1,0:T(8,128)(2,1)S(1)} %fusion.6), kind=kOutput, calls=%fused_computation.74 | convolution fusion | flops 2684354560 | bytes 12320768 | tf_op jit(solution)/shard_map/dot_general | solution.py:32
  96.5 8.9 %fusion.17 = f32[2048,1024]{1,0:T(8,128)} fusion(bf16[640,2048]{1,0:T(8,128)(2,1)} %get-tuple-element.19, bf16[640,1024]{1,0:T(8,128)(2,1)} %bitcast.61, f32[640]{0:T(1024)S(1)} %reshape.148), kind=kOutput, calls=%fused_computation.24 | convolution fusion | flops 2686320640 | bytes 12323328 | tf_op jit(solution)/shard_map/dot_general | solution.py:33
  105.4 43.9 %all-reduce.1 = (f32[8]{0:T(128)S(1)}, f32[8]{0:T(128)S(1)}) all-reduce(f32[8]{0:T(128)S(1)} %get-tuple-element.24, f32[8]{0:T(128)S(1)} %get-tuple-element.15), channel_id=1, replica_groups=mesh['expert'=8,'dp'=4] {'expert','dp'}, use_global_device_ids=true, to_apply=%region_16.17 | all-reduce | flops 16 | bytes 128 | tf_op jit(solution)/shard_map/psum | solution.py:61
  151.2 0.6 multiply_reduce_fusion.3
  152.5 0.6 reduce_sum.157
  154.4 0.6 multiply_reduce_fusion.4
  155.7 6.4 %fusion.13 = bf16[640,1024]{1,0:T(8,128)(2,1)} fusion(bf16[640,2048]{1,0:T(8,128)(2,1)S(1)} %fusion.6, bf16[1,1024,2048]{2,1,0:T(8,128)(2,1)} %param.15), kind=kOutput, calls=%fused_computation.19 | convolution fusion | flops 2685009920 | bytes 8126464 | tf_op jit(solution)/shard_map/dot_general | solution.py:41
  162.1 3.9 all-to-all-start.3
  166.5 52.9 %all-reduce = (f32[1024,8]{0,1:T(8,128)}, f32[8]{0:T(128)}) all-reduce(f32[1024,8]{0,1:T(8,128)S(1)} %convolution_bitcast_fusion, f32[8]{0:T(128)S(1)} %get-tuple-element.13), channel_id=1, replica_groups=mesh['expert'=8,'dp'=4] {'expert','dp'}, use_global_device_ids=true, to_apply=%region_22.23 | all-reduce | flops 8200 | bytes 65600 | tf_op jit(solution)/shard_map/psum | solution.py:133
  220.0 1.1 fusion.21
  221.1 21.5 %reduce-scatter.3.cloned.1.call-done = f32[1024,512]{1,0:T(8,128)} async-done(((f32[1024,2048]{1,0:T(8,128)}), f32[1024,512]{1,0:T(8,128)}) %reduce-scatter.3.cloned.1.call-update) | async-done | bytes 2097168 | tf_op jit(solution)/shard_map/reduce_scatter | solution.py:103
  242.6 2.7 convert_bitcast_fusion.1
  245.3 144.8 %reduce-scatter.5.cloned.1.call-done = f32[512,1024]{1,0:T(8,128)} async-done(((f32[2048,1024]{1,0:T(8,128)}), f32[512,1024]{1,0:T(8,128)}) %reduce-scatter.5.cloned.1.call-update) | async-done | bytes 2097168 | tf_op jit(solution)/shard_map/reduce_scatter | solution.py:104
  390.1 2.7 convert_bitcast_fusion
  (61 shorter events, 5.0 us)
Async XLA Ops:
  7.2 3.9 copy-start
  7.2 10.8 %copy-start.8 = (f32[256,8]{0,1:T(8,128)S(1)}, f32[256,8]{0,1:T(8,128)}, u32[]{:S(2)}) copy-start(f32[256,8]{0,1:T(8,128)} %param.12) | copy-start | bytes 24580
  7.2 10.8 %copy-start.10 = (f32[8]{0:T(128)S(1)}, f32[8]{0:T(128)}, u32[]{:S(2)}) copy-start(f32[8]{0:T(128)} %param.11) | copy-start | bytes 100
  7.2 10.8 %copy-start.6 = (bf16[1024,8]{0,1:T(8,128)(2,1)S(1)}, bf16[1024,8]{0,1:T(8,128)(2,1)}, u32[]{:S(2)}) copy-start(bf16[1024,8]{0,1:T(8,128)(2,1)} %param.10) | copy-start | bytes 49156
  7.2 11.1 %copy-start.5 = (bf16[256,1024]{1,0:T(8,128)(2,1)S(1)}, bf16[256,1024]{1,0:T(8,128)(2,1)}, u32[]{:S(2)}) copy-start(bf16[256,1024]{1,0:T(8,128)(2,1)} %param.17) | copy-start | bytes 1572868
  12.7 27.1 %copy-start.9 = (s32[256]{0:T(256)S(1)}, s32[256]{0:T(256)}, u32[]{:S(2)}) copy-start(s32[256]{0:T(256)} %param.14) | copy-start | bytes 3076
  12.7 23.5 %all-to-all-start.2 = ((bf16[8,80,1024]{2,1,0:T(8,128)(2,1)}), bf16[8,80,1024]{2,1,0:T(8,128)(2,1)S(1)}, u32[]{:S(2)}, u32[]{:S(2)}) async-start(bf16[8,80,1024]{2,1,0:T(8,128)(2,1)} %bitcast.6), calls=%async_computation.2 | async-start | bytes 2621440 | tf_op jit(solution)/shard_map/all_to_all | solution.py:90
  36.2 12.7 %copy-start.1 = (bf16[8,80,1024]{2,1,0:T(8,128)(2,1)}, bf16[8,80,1024]{2,1,0:T(8,128)(2,1)S(1)}, u32[]{:S(2)}) copy-start(bf16[8,80,1024]{2,1,0:T(8,128)(2,1)S(1)} %all-to-all-done.2) | copy-start | bytes 3932164
  36.2 21.7 %all-to-all-start.1 = ((bf16[8,80,1024]{2,1,0:T(8,128)(2,1)}), bf16[8,80,1024]{2,1,0:T(8,128)(2,1)S(1)}, u32[]{:S(2)}, u32[]{:S(2)}) async-start(bf16[8,80,1024]{2,1,0:T(8,128)(2,1)} %bitcast.3), calls=%async_computation.1 | async-start | bytes 2621440 | tf_op jit(solution)/shard_map/all_to_all | solution.py:91
  57.9 8.8 %copy-start.3 = (bf16[8,80,1024]{2,1,0:T(8,128)(2,1)}, bf16[8,80,1024]{2,1,0:T(8,128)(2,1)S(1)}, u32[]{:S(2)}) copy-start(bf16[8,80,1024]{2,1,0:T(8,128)(2,1)S(1)} %all-to-all-done.1) | copy-start | bytes 3932164
  57.9 13.0 %copy-start.4 = (pred[512,640]{1,0:T(8,128)(4,1)S(1)}, pred[512,640]{1,0:T(8,128)(4,1)}, u32[]{:S(2)}) copy-start(pred[512,640]{1,0:T(8,128)(4,1)} %iota_compare_fusion) | copy-start | bytes 983044
  57.9 18.4 %copy-start.7 = (s32[256,2]{0,1:T(2,128)S(1)}, s32[256,2]{0,1:T(2,128)}, u32[]{:S(2)}) copy-start(s32[256,2]{0,1:T(2,128)} %param.13) | copy-start | bytes 6148
  67.4 7.9 %all-to-all-start.4 = ((bf16[8,1,80]{2,1,0:T(2,128)(2,1)}), bf16[8,1,80]{2,1,0:T(2,128)(2,1)S(1)}, u32[]{:S(2)}, u32[]{:S(2)}) async-start(bf16[8,1,80]{2,1,0:T(2,128)(2,1)} %convert_element_type.106), calls=%async_computation.4 | async-start | bytes 8192 | tf_op jit(solution)/shard_map/all_to_all | solution.py:110
  70.7 171.9 %reduce-scatter.3.cloned.1.call-start = ((), (), s32[]{:S(2)}) async-start(), calls=%async_computation.7 | async-start | bytes 10485760 | tf_op jit(solution)/shard_map/reduce_scatter | solution.py:103
  84.3 6.5 %copy-start.2 = (bf16[8,80,1024]{2,1,0:T(8,128)(2,1)S(1)}, bf16[8,80,1024]{2,1,0:T(8,128)(2,1)}, u32[]{:S(2)}) copy-start(bf16[8,80,1024]{2,1,0:T(8,128)(2,1)} %copy-done.1) | copy-start | bytes 3932164
  96.4 293.7 %reduce-scatter.5.cloned.1.call-start = ((), (), s32[]{:S(2)}) async-start(), calls=%async_computation.8 | async-start | bytes 10485760 | tf_op jit(solution)/shard_map/reduce_scatter | solution.py:104
  162.1 57.3 %all-to-all-start.3 = ((bf16[8,80,1024]{2,1,0:T(8,128)(2,1)}), bf16[8,80,1024]{2,1,0:T(8,128)(2,1)S(1)}, u32[]{:S(2)}, u32[]{:S(2)}) async-start(bf16[8,80,1024]{2,1,0:T(8,128)(2,1)} %bitcast.62), calls=%async_computation.3 | async-start | bytes 2621440 | tf_op jit(solution)/shard_map/all_to_all | solution.py:109
Sparse Core Ops, SparseCore 0:
  96.6 146.0 reduce-scatter.2
  245.0 145.1 reduce-scatter.4
where the time goes:
time: 400 us
  waiting for transfers between devices  196 us (49%)
  blocking collectives  104 us (26%)
  matrix products  43.4 us (11%)
  other arithmetic  19.1 us (5%)
  between operations  18.2 us (5%)
  starting transfers between devices  16.2 us (4%)
    reduce_scatter x1, waiting for transfers between devices, on_device(): lax.psum_scatter(second_grad, 'dp', scatter_dimension=0, tiled=True)  145 us
    psum x1, blocking collectives, on_device(): lax.psum((weight_part, jnp.sum(logit_grad, axis=0)), ('expert', 'dp'))  52.9 us
    psum x1, blocking collectives, on_device(): lax.psum((jnp.sum(probs, axis=0), jnp.sum(0.5 * (1.0 + lax.erf(zscore * i...  43.9 us
    reduce_scatter x1, waiting for transfers between devices, on_device(): lax.psum_scatter(first_grad, 'dp', scatter_dimension=1, tiled=True)  21.5 us
    all_to_all x1, waiting for transfers between devices, on_device(): lax.all_to_all(sent_in, 'expert', split_axis=0, concat_axis=0, tiled=True)  16.3 us
    all_to_all x1, waiting for transfers between devices, on_device(): lax.all_to_all(sent_grad, 'expert', split_axis=0, concat_axis=0, tiled=True)  9.05 us
    dot_general x1, matrix products, expert_local(): jnp.dot(active_low.T, scaled_grad, preferred_element_type=jnp.float32)  8.86 us
    dot_general x1, matrix products, expert_local(): jnp.dot(rows_grad, w_second.T, preferred_element_type=jnp.float32)  8.76 us
  transfers between devices with their start and end apart: 6, of which 5 were waited for; matrix products, arithmetic and copies ran while one was open for 9% of the time, Pallas kernels for 0%

commit v1 on v0

--- a/solution.py
+++ b/solution.py
@@ -7,6 +7,29 @@
 aux_weight = 1.0
 inv_root_two = 0.7071067811865476
 inv_root_tau = 0.3989422804014327
+
+
+def in_blocks(x, dim, peers):
+    shape = x.shape
+    tiles = x.reshape(*shape[:dim], peers, shape[dim] // peers, *shape[dim + 1 :])
+    return jnp.moveaxis(tiles, dim, 0)
+
+
+def in_order(pieces, dim):
+    pieces = jnp.moveaxis(pieces, 0, dim)
+    shape = pieces.shape
+    return pieces.reshape(*shape[:dim], shape[dim] * shape[dim + 1], *shape[dim + 2 :])
+
+
+def swapped_with_each(x, axis, split_dim, concat_dim):
+    peers, mine = (lax.axis_size(axis), lax.axis_index(axis))
+    blocks = in_blocks(x, split_dim, peers)
+    finished = [blocks[mine]]
+    for hop in range(1, peers):
+        sent = blocks[mine ^ hop]
+        finished.append(lax.ppermute(sent, axis, [(i, i ^ hop) for i in range(peers)]))
+    blocks = jnp.stack(finished)[mine ^ jnp.arange(peers)]
+    return in_order(blocks, concat_dim)
 
 
 def gelu_tanh(values):
@@ -87,7 +110,7 @@
         .reshape(experts, capacity)
     )
     recv_in, recv_grad, recv_gate = (
-        lax.all_to_all(sent_in, "expert", split_axis=0, concat_axis=0, tiled=True),
+        swapped_with_each(sent_in, "expert", 0, 0),
         lax.all_to_all(sent_grad, "expert", split_axis=0, concat_axis=0, tiled=True),
         lax.all_to_all(sent_gate, "expert", split_axis=0, concat_axis=0, tiled=True),
     )

time: 400 us -> 403 us (level)
  waiting for transfers between devices: 196 us -> 186 us
  local copies, waits for them, and re-layouts: 3.41 us -> 10.8 us
    all_to_all x1 -> x0, waiting for transfers between devices: 16.3 us -> none  [on_device(): lax.all_to_all(sent_in, 'expert', split_axis=0, concat_axis=0, tiled=True)]
    ppermute x0 -> x7, waiting for transfers between devices: none -> 15.5 us  [swapped_with_each(): lax.ppermute(sent, axis, [(i, i ^ hop) for i in range(peers)])]
    all_to_all x1, waiting for transfers between devices: 9.05 us -> 0.01 us  [on_device(): lax.all_to_all(sent_grad, 'expert', split_axis=0, concat_axis=0, tiled=True)]
    ppermute x0 -> x7, starting transfers between devices: none -> 7.97 us  [swapped_with_each(): lax.ppermute(sent, axis, [(i, i ^ hop) for i in range(peers)])]
    all_to_all x1 -> x0, starting transfers between devices: 5.33 us -> none  [on_device(): lax.all_to_all(sent_in, 'expert', split_axis=0, concat_axis=0, tiled=True)]
    unnamed x23 -> x25, local copies, waits for them, and re-layouts: 0.94 us -> 5.56 us
  transfers between devices with their start and end apart: 6 -> 12, of which waited for: 5 -> 5; matrix products, arithmetic and copies ran while one was open for 9% -> 11% of each run, Pallas kernels for 0% -> 0%
where the time goes in v1:
time: 403 us; the launch traced here: 402 us
  waiting for transfers between devices  186 us (46%)
  blocking collectives  104 us (26%)
  matrix products  44.8 us (11%)
  starting transfers between devices  19.2 us (5%)
  other arithmetic  19.1 us (5%)
  between operations  18.3 us (5%)
  local copies, waits for them, and re-layouts  10.8 us (3%)
    reduce_scatter x1, waiting for transfers between devices, on_device(): lax.psum_scatter(second_grad, 'dp', scatter_dimension=0, tiled=True)  145 us
    psum x1, blocking collectives, on_device(): lax.psum((weight_part, jnp.sum(logit_grad, axis=0)), ('expert', 'dp'))  52.9 us
    psum x1, blocking collectives, on_device(): lax.psum((jnp.sum(probs, axis=0), jnp.sum(0.5 * (1.0 + lax.erf(zscore * i...  43.9 us
    reduce_scatter x1, waiting for transfers between devices, on_device(): lax.psum_scatter(first_grad, 'dp', scatter_dimension=1, tiled=True)  21.5 us
    ppermute x7, waiting for transfers between devices, swapped_with_each(): lax.ppermute(sent, axis, [(i, i ^ hop) for i in range(peers)])  15.5 us
    dot_general x1, matrix products, expert_local(): hidden = jnp.dot(rows_in, w_first, preferred_element_type=jnp.float32)  9.44 us
    dot_general x1, matrix products, expert_local(): jnp.dot(active_low.T, scaled_grad, preferred_element_type=jnp.float32)  8.86 us
    dot_general x1, matrix products, expert_local(): jnp.dot(rows_grad, w_second.T, preferred_element_type=jnp.float32)  8.75 us
  transfers between devices with their start and end apart: 12, of which 5 were waited for; matrix products, arithmetic and copies ran while one was open for 11% of the time, Pallas kernels for 0%

profile of v1, /device:TPU:0, one launch (start us, length us, event | category | flops | bytes accessed | tf_op | source)
XLA Modules:
  0.0 401.8 jit_solution(2803547650680044972)
XLA Ops:
  8.4 1.1 reduce-window.6
  11.6 1.0 dynamic-slice_bitcast_fusion
  13.2 2.6 collective-permute-start.1
  15.8 1.8 collective-permute-start.3
  17.6 2.7 convolution_convert_fusion.1
  20.2 3.9 all-to-all-start.1
  24.2 1.0 iota_compare_fusion
  25.5 3.0 collective-permute-start.5
  29.5 0.9 bitcast_dynamic-update-slice_fusion.5
  30.4 0.9 bitcast_dynamic-update-slice_fusion.4
  31.4 0.9 bitcast_dynamic-update-slice_fusion.3
  32.3 0.9 bitcast_dynamic-update-slice_fusion.2
  33.3 13.2 %collective-permute-done.5 = bf16[1,80,1024]{2,1,0:T(8,128)(2,1)S(1)} collective-permute-done((bf16[1,80,1024]{2,1,0:T(8,128)(2,1)}, bf16[1,80,1024]{2,1,0:T(8,128)(2,1)S(1)}, u32[]{:S(2)}, u32[]{:S(2)}) %collective-permute-start.5) | collective-permute-done | bytes 163872 | tf_op jit(solution)/shard_map/ppermute | solution.py:30
  46.4 2.3 collective-permute-done.6
  48.8 1.7 gather_fusion
  50.5 9.4 %multiply_convert_fusion = (bf16[640,2048]{1,0:T(8,128)(2,1)}, f32[640,2048]{1,0:T(8,128)}) fusion(bf16[640,1024]{1,0:T(8,128)(2,1)} %bitcast.94, bf16[1,1024,2048]{2,1,0:T(8,128)(2,1)} %param.15), kind=kOutput, calls=%fused_computation.11 | convolution fusion | flops 2696151040 | bytes 13369344 | tf_op jit(solution)/shard_map/dot_general | solution.py:47
  60.0 8.8 %multiply_reduce_fusion = (bf16[640]{0:T(1024)(128)(2,1)S(1)}, f32[640,2048]{1,0:T(8,128)}) fusion(bf16[640,2048]{1,0:T(8,128)(2,1)} %get-tuple-element.27, bf16[640,1024]{1,0:T(8,128)(2,1)S(1)} %bitcast.91, bf16[1,2048,1024]{2,1,0:T(8,128)(2,1)} %param.16), kind=kOutput, calls=%fused_computation.10 | convolution fusion | flops 2688286208 | bytes 13370624 | tf_op jit(solution)/shard_map/dot_general | solution.py:50
  69.4 3.3 all-to-all-start.3
  73.4 3.9 all-to-all-done.3
  79.2 7.1 %all_to_all.26 = bf16[8,1,80]{2,1,0:T(2,128)(2,1)S(1)} all-to-all(bf16[8,1,80]{2,1,0:T(2,128)(2,1)S(1)} %all_to_all.21), channel_id=1, replica_groups=mesh['expert'=8,'dp'=4] {'expert'}, dimensions={0} | all-to-all | bytes 2560 | tf_op jit(solution)/shard_map/all_to_all | solution.py:115
  86.3 6.5 %fusion.6 = bf16[640,2048]{1,0:T(8,128)(2,1)S(1)} fusion(f32[640,2048]{1,0:T(8,128)} %get-tuple-element.28, f32[640,2048]{1,0:T(8,128)} %get-tuple-element.30, f32[640]{0:T(1024)S(1)} %reshape.156), kind=kLoop, calls=%fused_computation.9 | loop fusion | flops 27525120 | bytes 13109760 | tf_op jit(solution)/shard_map/convert_element_type | solution.py:53
  92.8 5.7 %fusion.41 = f32[1024,2048]{1,0:T(8,128)} fusion(bf16[640,1024]{1,0:T(8,128)(2,1)S(1)} %bitcast.95, bf16[640,2048]{1,0:T(8,128)(2,1)S(1)} %fusion.6), kind=kOutput, calls=%fused_computation.93 | convolution fusion | flops 2684354560 | bytes 12320768 | tf_op jit(solution)/shard_map/dot_general | solution.py:55
  98.6 8.9 %fusion.17 = f32[2048,1024]{1,0:T(8,128)} fusion(bf16[640,2048]{1,0:T(8,128)(2,1)} %get-tuple-element.27, bf16[640,1024]{1,0:T(8,128)(2,1)} %bitcast.92, f32[640]{0:T(1024)S(1)} %reshape.156), kind=kOutput, calls=%fused_computation.25 | convolution fusion | flops 2686320640 | bytes 12323328 | tf_op jit(solution)/shard_map/dot_general | solution.py:56
  107.5 43.9 %all-reduce.1 = (f32[8]{0:T(128)S(1)}, f32[8]{0:T(128)S(1)}) all-reduce(f32[8]{0:T(128)S(1)} %get-tuple-element.32, f32[8]{0:T(128)S(1)} %get-tuple-element.15), channel_id=1, replica_groups=mesh['expert'=8,'dp'=4] {'expert','dp'}, use_global_device_ids=true, to_apply=%region_16.17 | all-reduce | flops 16 | bytes 128 | tf_op jit(solution)/shard_map/psum | solution.py:84
  157.7 6.4 %fusion.13 = bf16[640,1024]{1,0:T(8,128)(2,1)} fusion(bf16[640,2048]{1,0:T(8,128)(2,1)S(1)} %fusion.6, bf16[1,1024,2048]{2,1,0:T(8,128)(2,1)} %param.15), kind=kOutput, calls=%fused_computation.20 | convolution fusion | flops 2685009920 | bytes 8126464 | tf_op jit(solution)/shard_map/dot_general | solution.py:64
  164.1 3.9 all-to-all-start.2
  168.5 52.9 %all-reduce = (f32[1024,8]{0,1:T(8,128)}, f32[8]{0:T(128)}) all-reduce(f32[1024,8]{0,1:T(8,128)S(1)} %convolution_bitcast_fusion, f32[8]{0:T(128)S(1)} %get-tuple-element.13), channel_id=1, replica_groups=mesh['expert'=8,'dp'=4] {'expert','dp'}, use_global_device_ids=true, to_apply=%region_22.23 | all-reduce | flops 8200 | bytes 65600 | tf_op jit(solution)/shard_map/psum | solution.py:156
  222.0 1.1 fusion.21
  223.2 21.5 %reduce-scatter.3.cloned.1.call-done = f32[1024,512]{1,0:T(8,128)} async-done(((f32[1024,2048]{1,0:T(8,128)}), f32[1024,512]{1,0:T(8,128)}) %reduce-scatter.3.cloned.1.call-update) | async-done | bytes 2097168 | tf_op jit(solution)/shard_map/reduce_scatter | solution.py:126
  244.7 2.7 convert_bitcast_fusion.1
  247.4 144.8 %reduce-scatter.5.cloned.1.call-done = f32[512,1024]{1,0:T(8,128)} async-done(((f32[2048,1024]{1,0:T(8,128)}), f32[512,1024]{1,0:T(8,128)}) %reduce-scatter.5.cloned.1.call-update) | async-done | bytes 2097168 | tf_op jit(solution)/shard_map/reduce_scatter | solution.py:127
  392.2 2.7 convert_bitcast_fusion
  (80 shorter events, 12.1 us)
Async XLA Ops:
  7.2 3.9 copy-start
  12.6 12.5 %copy-start.4 = (bf16[1024,8]{0,1:T(8,128)(2,1)S(1)}, bf16[1024,8]{0,1:T(8,128)(2,1)}, u32[]{:S(2)}) copy-start(bf16[1024,8]{0,1:T(8,128)(2,1)} %param.10) | copy-start | bytes 49156
  12.6 12.5 %copy-start.6 = (f32[256,8]{0,1:T(8,128)S(1)}, f32[256,8]{0,1:T(8,128)}, u32[]{:S(2)}) copy-start(f32[256,8]{0,1:T(8,128)} %param.12) | copy-start | bytes 24580
  12.6 12.5 %copy-start.8 = (f32[8]{0:T(128)S(1)}, f32[8]{0:T(128)}, u32[]{:S(2)}) copy-start(f32[8]{0:T(128)} %param.11) | copy-start | bytes 100
  12.6 12.8 %collective-permute-start = (bf16[1,80,1024]{2,1,0:T(8,128)(2,1)}, bf16[1,80,1024]{2,1,0:T(8,128)(2,1)}, u32[]{:S(2)}, u32[]{:S(2)}) collective-permute-start(bf16[1,80,1024]{2,1,0:T(8,128)(2,1)} %get-tuple-element.25), channel_id=1, source_target_pairs={{0,4},{4,0},{8,12},{12,8},{16,20},{20,16},{24,28},{28,24},{1,5},{5... | collective-permute-start | bytes 491528 | tf_op jit(solution)/shard_map/ppermute | solution.py:30
  13.2 16.2 %collective-permute-start.1 = (bf16[1,80,1024]{2,1,0:T(8,128)(2,1)}, bf16[1,80,1024]{2,1,0:T(8,128)(2,1)}, u32[]{:S(2)}, u32[]{:S(2)}) collective-permute-start(bf16[1,80,1024]{2,1,0:T(8,128)(2,1)} %get-tuple-element.24), channel_id=1, source_target_pairs={{0,8},{4,12},{8,0},{12,4},{16,24},{20,28},{24,16},{28,20},{1,9},{5... | collective-permute-start | bytes 491528 | tf_op jit(solution)/shard_map/ppermute | solution.py:30
  15.8 14.7 %collective-permute-start.2 = (bf16[1,80,1024]{2,1,0:T(8,128)(2,1)}, bf16[1,80,1024]{2,1,0:T(8,128)(2,1)}, u32[]{:S(2)}, u32[]{:S(2)}) collective-permute-start(bf16[1,80,1024]{2,1,0:T(8,128)(2,1)} %get-tuple-element.23), channel_id=1, source_target_pairs={{0,12},{4,8},{8,4},{12,0},{16,28},{20,24},{24,20},{28,16},{1,13},{... | collective-permute-start | bytes 491528 | tf_op jit(solution)/shard_map/ppermute | solution.py:30
  15.8 15.6 %collective-permute-start.3 = (bf16[1,80,1024]{2,1,0:T(8,128)(2,1)}, bf16[1,80,1024]{2,1,0:T(8,128)(2,1)}, u32[]{:S(2)}, u32[]{:S(2)}) collective-permute-start(bf16[1,80,1024]{2,1,0:T(8,128)(2,1)} %get-tuple-element.22), channel_id=1, source_target_pairs={{0,16},{4,20},{8,24},{12,28},{16,0},{20,4},{24,8},{28,12},{1,17},{... | collective-permute-start | bytes 491528 | tf_op jit(solution)/shard_map/ppermute | solution.py:30
  17.6 7.9 %copy-start.7 = (s32[256]{0:T(256)S(1)}, s32[256]{0:T(256)}, u32[]{:S(2)}) copy-start(s32[256]{0:T(256)} %param.14) | copy-start | bytes 3076
  17.6 14.7 %collective-permute-start.4 = (bf16[1,80,1024]{2,1,0:T(8,128)(2,1)}, bf16[1,80,1024]{2,1,0:T(8,128)(2,1)}, u32[]{:S(2)}, u32[]{:S(2)}) collective-permute-start(bf16[1,80,1024]{2,1,0:T(8,128)(2,1)} %get-tuple-element.21), channel_id=1, source_target_pairs={{0,20},{4,16},{8,28},{12,24},{16,4},{20,0},{24,12},{28,8},{1,21},{... | collective-permute-start | bytes 491528 | tf_op jit(solution)/shard_map/ppermute | solution.py:30
  20.2 39.8 %all-to-all-start.1 = ((bf16[8,80,1024]{2,1,0:T(8,128)(2,1)}), bf16[8,80,1024]{2,1,0:T(8,128)(2,1)S(1)}, u32[]{:S(2)}, u32[]{:S(2)}) async-start(bf16[8,80,1024]{2,1,0:T(8,128)(2,1)} %bitcast.3), calls=%async_computation.1 | async-start | bytes 2621440 | tf_op jit(solution)/shard_map/all_to_all | solution.py:114
  25.5 20.9 %collective-permute-start.5 = (bf16[1,80,1024]{2,1,0:T(8,128)(2,1)}, bf16[1,80,1024]{2,1,0:T(8,128)(2,1)S(1)}, u32[]{:S(2)}, u32[]{:S(2)}) collective-permute-start(bf16[1,80,1024]{2,1,0:T(8,128)(2,1)} %get-tuple-element.20), channel_id=1, source_target_pairs={{0,24},{4,28},{8,16},{12,20},{16,8},{20,12},{24,0},{28,4},{1,25},{... | collective-permute-start | bytes 491528 | tf_op jit(solution)/shard_map/ppermute | solution.py:30
  29.4 19.4 %collective-permute-start.6 = (bf16[1,80,1024]{2,1,0:T(8,128)(2,1)}, bf16[1,80,1024]{2,1,0:T(8,128)(2,1)S(1)}, u32[]{:S(2)}, u32[]{:S(2)}) collective-permute-start(bf16[1,80,1024]{2,1,0:T(8,128)(2,1)} %get-tuple-element.19), channel_id=1, source_target_pairs={{0,28},{4,24},{8,20},{12,16},{16,12},{20,8},{24,4},{28,0},{1,29},{... | collective-permute-start | bytes 491528 | tf_op jit(solution)/shard_map/ppermute | solution.py:30
  60.0 8.8 %copy-start.1 = (bf16[8,80,1024]{2,1,0:T(8,128)(2,1)}, bf16[8,80,1024]{2,1,0:T(8,128)(2,1)S(1)}, u32[]{:S(2)}) copy-start(bf16[8,80,1024]{2,1,0:T(8,128)(2,1)S(1)} %all-to-all-done.1) | copy-start | bytes 3932164
  60.0 13.0 %copy-start.3 = (pred[512,640]{1,0:T(8,128)(4,1)S(1)}, pred[512,640]{1,0:T(8,128)(4,1)}, u32[]{:S(2)}) copy-start(pred[512,640]{1,0:T(8,128)(4,1)} %iota_compare_fusion) | copy-start | bytes 983044
  60.0 18.4 %copy-start.5 = (s32[256,2]{0,1:T(2,128)S(1)}, s32[256,2]{0,1:T(2,128)}, u32[]{:S(2)}) copy-start(s32[256,2]{0,1:T(2,128)} %param.13) | copy-start | bytes 6148
  69.4 7.9 %all-to-all-start.3 = ((bf16[8,1,80]{2,1,0:T(2,128)(2,1)}), bf16[8,1,80]{2,1,0:T(2,128)(2,1)S(1)}, u32[]{:S(2)}, u32[]{:S(2)}) async-start(bf16[8,1,80]{2,1,0:T(2,128)(2,1)} %convert_element_type.106), calls=%async_computation.3 | async-start | bytes 8192 | tf_op jit(solution)/shard_map/all_to_all | solution.py:133
  72.8 171.9 %reduce-scatter.3.cloned.1.call-start = ((), (), s32[]{:S(2)}) async-start(), calls=%async_computation.6 | async-start | bytes 10485760 | tf_op jit(solution)/shard_map/reduce_scatter | solution.py:126
  86.3 6.5 %copy-start.2 = (bf16[8,80,1024]{2,1,0:T(8,128)(2,1)S(1)}, bf16[8,80,1024]{2,1,0:T(8,128)(2,1)}, u32[]{:S(2)}) copy-start(bf16[8,80,1024]{2,1,0:T(8,128)(2,1)} %gather_fusion) | copy-start | bytes 3932164
  98.5 293.7 %reduce-scatter.5.cloned.1.call-start = ((), (), s32[]{:S(2)}) async-start(), calls=%async_computation.7 | async-start | bytes 10485760 | tf_op jit(solution)/shard_map/reduce_scatter | solution.py:127
  164.1 57.3 %all-to-all-start.2 = ((bf16[8,80,1024]{2,1,0:T(8,128)(2,1)}), bf16[8,80,1024]{2,1,0:T(8,128)(2,1)S(1)}, u32[]{:S(2)}, u32[]{:S(2)}) async-start(bf16[8,80,1024]{2,1,0:T(8,128)(2,1)} %bitcast.93), calls=%async_computation.2 | async-start | bytes 2621440 | tf_op jit(solution)/shard_map/all_to_all | solution.py:132
Sparse Core Ops, SparseCore 0:
  98.6 145.9 reduce-scatter.2
  247.0 145.1 reduce-scatter.4
